TPU v7x, 32 devices: a whole 2x2x4 slice. The times are simulated.
32 devices in a mesh: row: 8 (over y, x, core), col: 4 (over z).
Axes of the slice: x: 2, y: 2, z: 4, core: 2. Of those that a mesh axis runs over, the one named last changes fastest.
Arguments:
- covariance: bfloat16 [16384, 16384], P('row', 'col'), may hold values from -0.12 to 0.6, as said below
- estimate: bfloat16 [16384, 16384], P('row', 'col'), may hold values from -2.3 to 12, as said below
- dual_var: bfloat16 [16384, 16384], P('row', 'col'), may hold values from -1.7 to 1.7, as said below
- start_basis: float32 [16384, 128], P('row'), may hold values from -6 to 6
Outputs:
- next_estimate: float32 [16384, 16384], P('row', 'col')
- next_dual: bfloat16 [16384, 16384], P('row', 'col')
Inputs may be any that keep to these rules, and one draw needn't show every extreme that they name: `covariance`: symmetric. `estimate`: symmetric. `dual_var`: symmetric.
All inputs are finite; a program needn't handle non-finite values.
Results may differ from a plain program's by a relative error of at most 0.001.
Values sent between devices are 32-bit elements; how exact they have to be, the bound alone decides.
A program may use at most 192 MiB of HBM per device.

v0:
```python
import functools

import jax
import jax.numpy as jnp
from jax import lax
from jax.experimental import pallas as pl
from jax.experimental.pallas import tpu as pltpu
from jax.sharding import PartitionSpec as P

NS_ITERS = 12


penalty = 0.01
threshold = 0.2
base_level = 10.0
highest = lax.Precision.HIGHEST


def from_root(value, axis, source):
    kept = jnp.where(lax.axis_index(axis) == source, value, 0).astype(value.dtype)
    return lax.psum(kept, axis)


def inner_product(left_side, right_side):
    return lax.dot_general(
        left_side,
        right_side,
        (((0,), (0,)), ((), ())),
        precision=highest,
        preferred_element_type=jnp.float32,
    )


def normalize(mapped, gram_matrix):
    lower_factor = jnp.linalg.cholesky(gram_matrix)
    identity = jnp.eye(gram_matrix.shape[0], dtype=jnp.float32)
    inverse = lax.linalg.triangular_solve(lower_factor, identity, left_side=True, lower=True)
    return jnp.dot(mapped, inverse.T, precision=highest, preferred_element_type=jnp.float32)


def response_of(ritz_matrix):
    identity = jnp.eye(ritz_matrix.shape[0], dtype=jnp.float32)
    square = (
        jnp.dot(ritz_matrix, ritz_matrix, precision=highest, preferred_element_type=jnp.float32)
        + 4.0 * penalty * identity
    )
    frobenius = jnp.sqrt(jnp.sum(square * square))

    def newton(sweep_index, state_pair):
        iterate, partner = state_pair
        factor = 0.5 * (
            3.0 * identity
            - jnp.dot(partner, iterate, precision=highest, preferred_element_type=jnp.float32)
        )
        return (
            jnp.dot(iterate, factor, precision=highest, preferred_element_type=jnp.float32),
            jnp.dot(factor, partner, precision=highest, preferred_element_type=jnp.float32),
        )

    iterate, partner = lax.fori_loop(0, NS_ITERS, newton, (square / frobenius, identity))
    square_root = jnp.sqrt(frobenius) * iterate
    return (ritz_matrix + square_root) / (2.0 * penalty) - base_level * identity


def column_basis(shifted, row_basis):
    partial_terms = lax.dot_general(
        shifted,
        row_basis,
        (((0,), (0,)), ((), ())),
        precision=highest,
        preferred_element_type=jnp.float32,
    )
    mapped = lax.psum(partial_terms, "row")
    gram_matrix = lax.psum(inner_product(mapped, mapped), "col")
    return normalize(mapped, gram_matrix)


def row_image(shifted, col_basis):
    local_terms = jnp.dot(shifted, col_basis, precision=highest, preferred_element_type=jnp.float32)
    return lax.psum(local_terms, "col")


def row_inner(left_side, right_side):
    return lax.psum(inner_product(left_side, right_side), "row")


def plain_body(covariance, estimate, dual_var, start_basis):
    shifted = penalty * (
        estimate.astype(jnp.float32) - dual_var.astype(jnp.float32)
    ) - covariance.astype(jnp.float32)
    rows_tile = shifted.shape[0]
    cols_tile = shifted.shape[1]
    row_basis = start_basis
    col_basis = column_basis(shifted, row_basis)
    blocks_per_column = lax.axis_size("row") // lax.axis_size("col")
    row_index = lax.axis_index("row")
    own_block = lax.dynamic_slice_in_dim(
        col_basis, row_index % blocks_per_column * rows_tile, rows_tile, 0
    )
    row_basis = from_root(own_block, "col", row_index // blocks_per_column)
    product = row_image(shifted, col_basis)
    raw_ritz = row_inner(row_basis, product)
    ritz_matrix = 0.5 * (raw_ritz + raw_ritz.T)
    response = response_of(ritz_matrix)
    weighted = jnp.dot(row_basis, response, precision=highest, preferred_element_type=jnp.float32)
    theta_tile = lax.dot_general(
        weighted,
        col_basis,
        (((1,), (1,)), ((), ())),
        precision=highest,
        preferred_element_type=jnp.float32,
    )
    row_ids = row_index * rows_tile + lax.broadcasted_iota(jnp.int32, (rows_tile, 1), 0)
    col_ids = lax.axis_index("col") * cols_tile + lax.broadcasted_iota(jnp.int32, (1, cols_tile), 1)
    theta_tile = theta_tile + jnp.where(row_ids == col_ids, base_level, 0.0)
    mixture = theta_tile + dual_var.astype(jnp.float32)
    clipped = jnp.clip(mixture, -threshold, threshold)
    return (mixture - clipped, clipped.astype(jnp.bfloat16))


MESH = pl.DeviceIdType.MESH
VMEM = pl.BlockSpec(memory_space=pltpu.VMEM)
VMEM_BYTES = 60 * 1024 * 1024


def high_dot(left_side, right_side, dims):
    return lax.dot_general(
        left_side, right_side, (dims, ((), ())), precision=highest, preferred_element_type=jnp.float32
    )


def split(value):
    upper = value.astype(jnp.bfloat16)
    return upper, (value - upper.astype(jnp.float32)).astype(jnp.bfloat16)


def fill_left(left_ref, index, basis_t):
    scaled_upper, scaled_lower = split(penalty * basis_t)
    upper, lower = split(basis_t)
    half = basis_t.shape[0]
    left_ref[0, index, :half] = scaled_upper
    left_ref[0, index, half:] = scaled_lower
    left_ref[1, index, :half] = -scaled_upper
    left_ref[1, index, half:] = -scaled_lower
    left_ref[2, index, :half] = -upper
    left_ref[2, index, half:] = -lower


def shifted_product(left_ref, tiles, acc_ref):
    blocks, depth = left_ref.shape[1], left_ref.shape[3]
    acc_ref[...] = jnp.zeros_like(acc_ref)

    def step(block, carry):
        rows = pl.ds(pl.multiple_of(block * depth, depth), depth)
        total = acc_ref[...]
        for which, tile in enumerate(tiles):
            total += jnp.dot(
                left_ref[which, block], tile[rows, :], preferred_element_type=jnp.float32
            )
        acc_ref[...] = total
        return carry

    lax.fori_loop(0, blocks, step, 0)
    half = acc_ref.shape[0] // 2
    return acc_ref[:half] + acc_ref[half:]


def image_kernel(est_ref, dual_ref, cov_ref, basis_ref, out_ref, left_ref, acc_ref):
    depth = left_ref.shape[3]

    @pl.when(pl.program_id(0) == 0)
    def _():
        for index in range(left_ref.shape[1]):
            fill_left(left_ref, index, basis_ref[index * depth : (index + 1) * depth, :].T)

    out_ref[0] = shifted_product(left_ref, (est_ref, dual_ref, cov_ref), acc_ref)


def moment_kernel(est_ref, dual_ref, cov_ref, rows_ref, cols_ref, out_ref, left_ref, acc_ref):
    step = pl.program_id(0)
    rank = rows_ref.shape[1]

    @pl.when(step == 0)
    def _():
        for index in range(left_ref.shape[1]):
            fill_left(left_ref, index, rows_ref[index])
        own = cols_ref[lax.axis_index("row")]
        out_ref[:rank] = high_dot(own, own, ((1,), (1,)))
        out_ref[rank:] = jnp.zeros((rank, rank), jnp.float32)

    image = shifted_product(left_ref, (est_ref, dual_ref, cov_ref), acc_ref)
    out_ref[rank:] += high_dot(image, cols_ref[step], ((1,), (1,)))


def local_call(kernel, matrices, extras, piece, depth, out_shape, out_spec):
    rows_tile, cols_tile = matrices[0].shape
    rank = 128
    tile_spec = pl.BlockSpec((rows_tile, piece), lambda step: (0, step))
    whole = [pl.BlockSpec(extra.shape, functools.partial(lambda n, step: (0,) * n, extra.ndim)) for extra in extras]
    rank = extras[0].shape[1]
    return pl.pallas_call(
        kernel,
        grid=(cols_tile // piece,),
        in_specs=[tile_spec] * 3 + whole,
        out_specs=out_spec,
        out_shape=out_shape,
        scratch_shapes=[
            pltpu.VMEM((3, rows_tile // depth, 2 * rank, depth), jnp.bfloat16),
            pltpu.VMEM((2 * rank, piece), jnp.float32),
        ],
        compiler_params=pltpu.CompilerParams(
            dimension_semantics=("arbitrary",), vmem_limit_bytes=VMEM_BYTES
        ),
    )(*matrices, *extras)


def spread_kernel(n_row, n_col, part_ref, mc_ref, mr_ref, near, other, zbuf, sems):
    row, col = lax.axis_index("row"), lax.axis_index("col")
    chips = n_row // 2
    chip, core = row // 2, row % 2
    sibling = chip * 2 + 1 - core
    ratio = n_row // n_col
    group = n_row // ratio

    barrier = pltpu.get_barrier_semaphore()

    def greet_row(t, carry):
        pl.semaphore_signal(barrier, inc=1, device_id=((row + t) % n_row, col), device_id_type=MESH)
        return carry

    def greet_col(t, carry):
        pl.semaphore_signal(barrier, inc=1, device_id=(row, (col + t) % n_col), device_id_type=MESH)
        return carry

    lax.fori_loop(1, n_row, greet_row, 0)
    lax.fori_loop(1, n_col, greet_col, 0)
    pl.semaphore_wait(barrier, n_row - 1 + n_col - 1)

    send1, recv1, send2, recv2, send3, recv3, send4, recv4, send5, recv5, send6, recv6 = sems

    def copy(src, dst, send, recv, target):
        return pltpu.make_async_remote_copy(
            src_ref=src, dst_ref=dst, send_sem=send, recv_sem=recv, device_id=target, device_id_type=MESH
        )

    first = []
    for t in range(chips):
        there = (chip + 1 + t) % chips
        first.append(
            copy(part_ref.at[2 * there + 1 - core], near.at[t], send1.at[t], recv1.at[t], (sibling, col))
        )
        first[-1].start()
    second = []
    for t in range(chips):
        there = (chip + 1 + t) % chips
        first[t].wait_recv()
        if t < chips - 1:
            near[t] = near[t] + part_ref[2 * there + core]
            second.append(
                copy(near.at[t], other.at[t], send2.at[t], recv2.at[t], (2 * there + core, col))
            )
            second[-1].start()
    total = near[chips - 1] + part_ref[row]
    for t in range(chips - 1):
        second[t].wait_recv()
        total += other[t]
    mc_ref[row] = total

    own = mc_ref.at[row]
    along = []
    for t in range(n_col - 1):
        along.append(copy(own, zbuf.at[t], send4.at[t], recv4.at[t], (row, (col + 1 + t) % n_col)))
        along[-1].start()
    plane = []
    for t in range(chips - 1):
        there = (chip + 1 + t) % chips
        plane.append(copy(own, own, send3.at[t], recv3.at[t], (2 * there + core, col)))
        plane[-1].start()
    pair = [copy(own, own, send5.at[0], recv5.at[0], (sibling, col))]
    pair[0].start()

    slot = row % group
    onward = []
    for t in range(n_col - 1):
        source = (col + n_col - 1 - t) % n_col
        target = source * ratio + row // group
        along[t].wait_recv()
        hop = copy(zbuf.at[t], mr_ref.at[slot], send6.at[t], recv6.at[slot], (target, col))

        @pl.when(target != row)
        def _():
            hop.start()

        @pl.when(target == row)
        def _():
            mr_ref[slot] = zbuf[t]

        onward.append((hop, target))

    for t in range(chips - 1):
        source = 2 * ((chip + chips - 1 - t) % chips) + core
        arrived = mc_ref.at[source]
        copy(own, arrived, send3.at[t], recv3.at[t], (row, col)).wait_recv()
        pair.append(copy(arrived, arrived, send5.at[t + 1], recv5.at[t + 1], (sibling, col)))
        pair[-1].start()
    for t in range(chips):
        source = 2 * ((chip + chips - t) % chips) + 1 - core
        copy(own, mc_ref.at[source], send5.at[t], recv5.at[t], (sibling, col)).wait_recv()

    @pl.when(row // ratio == col)
    def _():
        for k in range(group):
            mr_ref[k] = mc_ref[(row % ratio) * group + k]

    for k in range(group):
        @pl.when((row // ratio != col) & ((row % ratio) * group + k != row))
        def _():
            copy(zbuf.at[0], mr_ref.at[k], send6.at[0], recv6.at[k], (sibling, col)).wait_recv()

    for item in first + second + along + plane + pair:
        item.wait_send()
    for hop, target in onward:
        @pl.when(target != row)
        def _():
            hop.wait_send()


def spread(parts, n_row, n_col):
    rank, piece = parts.shape[1:]
    chips, ratio = n_row // 2, n_row // n_col
    group = n_row // ratio
    dma = pltpu.SemaphoreType.DMA

    def kernel(part_ref, mc_ref, mr_ref, near, other, zbuf, *sems):
        spread_kernel(n_row, n_col, part_ref, mc_ref, mr_ref, near, other, zbuf, sems)

    return pl.pallas_call(
        kernel,
        in_specs=[VMEM],
        out_specs=(VMEM, VMEM),
        out_shape=(
            jax.ShapeDtypeStruct((n_row, rank, piece), jnp.float32),
            jax.ShapeDtypeStruct((group, rank, piece), jnp.float32),
        ),
        scratch_shapes=[
            pltpu.VMEM((chips, rank, piece), jnp.float32),
            pltpu.VMEM((chips - 1, rank, piece), jnp.float32),
            pltpu.VMEM((n_col - 1, rank, piece), jnp.float32),
            dma((chips,)), dma((chips,)),
            dma((chips - 1,)), dma((chips - 1,)),
            dma((chips - 1,)), dma((chips - 1,)),
            dma((n_col - 1,)), dma((n_col - 1,)),
            dma((chips,)), dma((chips,)),
            dma((n_col - 1,)), dma((group,)),
        ],
        compiler_params=pltpu.CompilerParams(
            collective_id=0, has_side_effects=True, vmem_limit_bytes=VMEM_BYTES
        ),
    )(parts)


def total_kernel(n_row, n_col, term_ref, out_ref, terms, send1, recv1, send2, recv2):
    count = n_row * n_col
    row, col = lax.axis_index("row"), lax.axis_index("col")
    me = row * n_col + col
    barrier = pltpu.get_barrier_semaphore()

    def place(t):
        there = (me + t) % count
        return there, (there // n_col, there % n_col)

    def greet(t, carry):
        pl.semaphore_signal(barrier, inc=1, device_id=place(t)[1], device_id_type=MESH)
        return carry

    lax.fori_loop(1, count, greet, 0)
    pl.semaphore_wait(barrier, count - 1)

    def scatter(t):
        there, target = place(t)
        return pltpu.make_async_remote_copy(
            src_ref=term_ref.at[there], dst_ref=terms.at[t], send_sem=send1.at[t],
            recv_sem=recv1.at[t], device_id=target, device_id_type=MESH,
        )

    def gather(t, slot):
        return pltpu.make_async_remote_copy(
            src_ref=out_ref.at[me], dst_ref=out_ref.at[slot], send_sem=send2.at[t],
            recv_sem=recv2.at[t], device_id=place(t)[1], device_id_type=MESH,
        )

    def each(action):
        def step(t, carry):
            action(t)
            return carry

        lax.fori_loop(1, count, step, 0)

    each(lambda t: scatter(t).start())
    terms[0] = term_ref[me]
    each(lambda t: scatter(t).wait_recv())
    out_ref[me] = jnp.sum(terms[...], axis=0)
    each(lambda t: gather(t, me).start())
    each(lambda t: gather(t, (me + count - t) % count).wait_recv())
    each(lambda t: scatter(t).wait_send())
    each(lambda t: gather(t, me).wait_send())


def total(terms, n_row, n_col):
    count = n_row * n_col
    blocks = terms.reshape(count, terms.shape[0] // count, terms.shape[1])
    dma = pltpu.SemaphoreType.DMA
    summed = pl.pallas_call(
        functools.partial(total_kernel, n_row, n_col),
        in_specs=[VMEM],
        out_specs=VMEM,
        out_shape=jax.ShapeDtypeStruct(blocks.shape, jnp.float32),
        scratch_shapes=[pltpu.VMEM(blocks.shape, jnp.float32)] + [dma((count,))] * 4,
        compiler_params=pltpu.CompilerParams(collective_id=1, has_side_effects=True),
    )(blocks)
    return summed.reshape(terms.shape)


def weight_kernel(moment_ref, rows_ref, out_ref, inverse_ref, ritz_ref, iterate_ref, partner_ref):
    rank = rows_ref.shape[1]
    row_ids = lax.broadcasted_iota(jnp.int32, (rank, rank), 0)
    col_ids = lax.broadcasted_iota(jnp.int32, (rank, rank), 1)
    line_ids = lax.broadcasted_iota(jnp.int32, (1, rank), 1)
    identity = jnp.where(row_ids == col_ids, 1.0, 0.0)
    inverse = moment_ref[:rank]
    for k in range(rank):
        pivot = 1.0 / inverse[k : k + 1, k : k + 1]
        column = inverse[:, k : k + 1]
        line = jnp.where(line_ids == k, 1.0, inverse[k : k + 1, :]) * pivot
        inverse = jnp.where(
            row_ids == k, line, jnp.where(col_ids == k, 0.0, inverse) - column * line
        )
    inverse_ref[...] = inverse
    raw = moment_ref[rank:]
    iterate_ref[...] = 0.5 * (raw + raw.T)
    plain = ((1,), (0,))
    ritz_ref[...] = high_dot(inverse_ref[...], iterate_ref[...], plain)
    square = high_dot(ritz_ref[...], ritz_ref[...], plain) + 4.0 * penalty * identity
    frobenius = jnp.sqrt(jnp.sum(square * square.T, keepdims=True))
    iterate_ref[...] = square / frobenius
    partner_ref[...] = identity

    def newton(step, carry):
        iterate, partner = iterate_ref[...], partner_ref[...]
        factor = 0.5 * (3.0 * identity - high_dot(partner, iterate, plain))
        iterate_ref[...] = high_dot(iterate, factor, plain)
        partner_ref[...] = high_dot(factor, partner, plain)
        return carry

    lax.fori_loop(0, NS_ITERS, newton, 0)
    root = jnp.sqrt(frobenius) * iterate_ref[...]
    response = (ritz_ref[...] + root) / (2.0 * penalty) - base_level * identity
    partner_ref[...] = high_dot(response, inverse_ref[...], plain)
    piece = rows_ref.shape[2]
    for k in range(rows_ref.shape[0]):
        out_ref[k * piece : (k + 1) * piece, :] = high_dot(rows_ref[k].T, partner_ref[...], plain)


def finish_kernel(weighted_ref, cols_ref, dual_ref, est_ref, clip_ref, right_ref, low_ref):
    step = pl.program_id(0)
    count, rank, piece = cols_ref.shape
    depth = dual_ref.shape[0]

    @pl.when(step == 0)
    def _():
        for k in range(count):
            upper, lower = split(cols_ref[k])
            right_ref[k, :rank] = upper
            right_ref[k, rank:] = upper
            low_ref[k] = lower

    upper, lower = split(weighted_ref[...])
    both = jnp.concatenate([upper, lower], axis=1)
    n_grid = pl.num_programs(0)
    row_start = (lax.axis_index("row") * n_grid + step) * depth
    gap = (
        lax.broadcasted_iota(jnp.int32, (depth, piece), 1)
        - lax.broadcasted_iota(jnp.int32, (depth, piece), 0)
    )
    for k in range(count):
        where = slice(k * piece, (k + 1) * piece)
        col_start = lax.axis_index("col") * (count * piece) + k * piece
        theta = jnp.dot(both, right_ref[k], preferred_element_type=jnp.float32)
        theta += jnp.dot(upper, low_ref[k], preferred_element_type=jnp.float32)
        theta += jnp.where(gap == row_start - col_start, base_level, 0.0)
        mixture = theta + dual_ref[:, where].astype(jnp.float32)
        clipped = jnp.clip(mixture, -threshold, threshold)
        est_ref[:, where] = mixture - clipped
        clip_ref[:, where] = clipped.astype(jnp.bfloat16)


def finish(weighted, cols, dual_var):
    rows_tile, cols_tile = dual_var.shape
    count, rank, piece = cols.shape
    depth = min(256, rows_tile)
    wide = pl.BlockSpec((depth, cols_tile), lambda step: (step, 0))
    return pl.pallas_call(
        finish_kernel,
        grid=(rows_tile // depth,),
        in_specs=[
            pl.BlockSpec((depth, rank), lambda step: (step, 0)),
            pl.BlockSpec(cols.shape, lambda step: (0, 0, 0)),
            wide,
        ],
        out_specs=(wide, wide),
        out_shape=(
            jax.ShapeDtypeStruct(dual_var.shape, jnp.float32),
            jax.ShapeDtypeStruct(dual_var.shape, jnp.bfloat16),
        ),
        scratch_shapes=[
            pltpu.VMEM((count, 2 * rank, piece), jnp.bfloat16),
            pltpu.VMEM((count, rank, piece), jnp.bfloat16),
        ],
        compiler_params=pltpu.CompilerParams(
            dimension_semantics=("arbitrary",), vmem_limit_bytes=VMEM_BYTES
        ),
    )(weighted, cols, dual_var)


def fast_body(n_row, n_col, covariance, estimate, dual_var, start_basis):
    rows_tile, cols_tile = covariance.shape
    rank = start_basis.shape[1]
    piece = cols_tile // n_row
    matrices = (estimate, dual_var, covariance)
    parts = local_call(
        image_kernel, matrices, (start_basis,), piece, piece,
        jax.ShapeDtypeStruct((n_row, rank, piece), jnp.float32),
        pl.BlockSpec((1, rank, piece), lambda step: (step, 0, 0)),
    )
    cols, rows = spread(parts, n_row, n_col)
    moments = local_call(
        moment_kernel, matrices, (rows, cols), piece, piece,
        jax.ShapeDtypeStruct((2 * rank, rank), jnp.float32),
        pl.BlockSpec((2 * rank, rank), lambda step: (0, 0)),
    )
    moments = total(moments, n_row, n_col)
    weighted = pl.pallas_call(
        weight_kernel,
        in_specs=[VMEM, VMEM],
        out_specs=VMEM,
        out_shape=jax.ShapeDtypeStruct((rows_tile, rank), jnp.float32),
        scratch_shapes=[pltpu.VMEM((rank, rank), jnp.float32)] * 4,
        compiler_params=pltpu.CompilerParams(vmem_limit_bytes=VMEM_BYTES),
    )(moments, rows)
    return finish(weighted, cols, dual_var)


def body(covariance, estimate, dual_var, start_basis):
    n_row, n_col = lax.axis_size("row"), lax.axis_size("col")
    rows_tile, cols_tile = covariance.shape
    rank = start_basis.shape[1]
    piece = cols_tile // n_row
    fits = (
        n_row % 2 == 0
        and n_row % n_col == 0
        and cols_tile % n_row == 0
        and piece % 128 == 0
        and rows_tile % piece == 0
        and rank % 128 == 0
        and 2 * rank % (8 * n_row * n_col) == 0
    )
    if not fits:
        return plain_body(covariance, estimate, dual_var, start_basis)
    return fast_body(n_row, n_col, covariance, estimate, dual_var, start_basis)


def solution(mesh):
    return jax.shard_map(
        body,
        mesh=mesh,
        in_specs=(P("row", "col"), P("row", "col"), P("row", "col"), P("row", None)),
        out_specs=(P("row", "col"), P("row", "col")),
        check_vma=False,
    )
```

profile of v0, /device:TPU:0, one launch (start us, length us, event | category | flops | bytes accessed | tf_op | source)
XLA Modules:
  0.0 178.1 jit_solution(7614363225130565510)
XLA Ops:
  0.6 26.0 %shard_map.59.part_ref = f32[8,128,512]{2,1,0:T(8,128)} custom-call(bf16[2048,4096]{1,0:T(8,128)(2,1)} %est_ref.3, bf16[2048,4096]{1,0:T(8,128)(2,1)} %dual_ref.5, bf16[2048,4096]{1,0:T(8,128)(2,1)} %cov_ref.3, f32[2048,128]{1,0:T(8,128)} %basis_ref.1), custom_call_target="tpu_custom_call" | custom-call | tf_op jit(solution)/shard_map/pallas_call | solution.py:201
  26.6 53.5 %shard_map.60 = (f32[8,128,512]{2,1,0:T(8,128)}, f32[4,128,512]{2,1,0:T(8,128)}) custom-call(f32[8,128,512]{2,1,0:T(8,128)} %shard_map.59.part_ref), custom_call_target="tpu_custom_call" | custom-call | tf_op jit(solution)/shard_map/pallas_call | solution.py:337
  80.1 28.3 %shard_map.61 = f32[256,128]{1,0:T(8,128)} custom-call(bf16[2048,4096]{1,0:T(8,128)(2,1)} %est_ref.3, bf16[2048,4096]{1,0:T(8,128)(2,1)} %dual_ref.5, bf16[2048,4096]{1,0:T(8,128)(2,1)} %cov_ref.3, f32[4,128,512]{2,1,0:T(8,128)} %get-tuple-element.4.rows_ref, f32[8,128,512]{2,1,0:T(8,128)} %get-tuple-element.5.cols_ref), custom_call_target="tpu_custom_call" | custom-call | tf_op jit(solution)/shard_map/pallas_call | solution.py:201
  108.4 23.7 %shard_map.62 = f32[32,8,128]{2,1,0:T(8,128)} custom-call(f32[32,8,128]{2,1,0:T(8,128)} %bitcast.2), custom_call_target="tpu_custom_call" | custom-call | tf_op jit(solution)/shard_map/pallas_call | solution.py:413
  132.2 20.4 %shard_map.63.weighted_ref = f32[2048,128]{1,0:T(8,128)} custom-call(f32[256,128]{1,0:T(8,128)} %bitcast.3, f32[4,128,512]{2,1,0:T(8,128)} %get-tuple-element.4.rows_ref), custom_call_target="tpu_custom_call" | custom-call | tf_op jit(solution)/shard_map/pallas_call | solution.py:542
  152.6 25.6 %shard_map.64 = (f32[2048,4096]{1,0:T(8,128)}, bf16[2048,4096]{1,0:T(8,128)(2,1)}) custom-call(f32[2048,128]{1,0:T(8,128)} %shard_map.63.weighted_ref, f32[8,128,512]{2,1,0:T(8,128)} %get-tuple-element.5.cols_ref, bf16[2048,4096]{1,0:T(8,128)(2,1)} %dual_ref.5), custom_call_target="tpu_custom_call" | custom-call | tf_op jit(solution)/shard_map/pallas_call | solution.py:502
where the time goes:
time: 179 us; the launch traced here: 178 us
  Pallas kernels  177 us (99%)
    pallas_call x2, Pallas kernels, local_call(): pl.pallas_call(kernel, grid=(cols_tile // piece,), in_specs=[tile_spec] *...  54.3 us
    pallas_call x1, Pallas kernels, spread(): pl.pallas_call(kernel, in_specs=[VMEM], out_specs=(VMEM, VMEM), out_shape...  53.5 us
    pallas_call x1, Pallas kernels, finish(): pl.pallas_call(finish_kernel, grid=(rows_tile // depth,), in_specs=[pl.Bl...  25.6 us
    pallas_call x1, Pallas kernels, total(): pl.pallas_call(functools.partial(total_kernel, n_row, n_col), in_specs=[V...  23.7 us
    pallas_call x1, Pallas kernels, fast_body(): pl.pallas_call(weight_kernel, in_specs=[VMEM, VMEM], out_specs=VMEM, out_...  20.4 us

commit v1 on v0

--- a/solution.py
+++ b/solution.py
@@ -134,84 +134,101 @@
     return upper, (value - upper.astype(jnp.float32)).astype(jnp.bfloat16)
 
 
-def fill_left(left_ref, index, basis_t):
-    scaled_upper, scaled_lower = split(penalty * basis_t)
-    upper, lower = split(basis_t)
-    half = basis_t.shape[0]
-    left_ref[0, index, :half] = scaled_upper
-    left_ref[0, index, half:] = scaled_lower
-    left_ref[1, index, :half] = -scaled_upper
-    left_ref[1, index, half:] = -scaled_lower
-    left_ref[2, index, :half] = -upper
-    left_ref[2, index, half:] = -lower
-
-
-def shifted_product(left_ref, tiles, acc_ref):
-    blocks, depth = left_ref.shape[1], left_ref.shape[3]
+def image_kernel(est_ref, dual_ref, cov_ref, basis_ref, out_ref, left_ref, acc_ref):
+    blocks, both, depth = left_ref.shape
+    half = both // 2
+
+    @pl.when(pl.program_id(0) == 0)
+    def _():
+        for index in range(blocks):
+            upper, lower = split(basis_ref[index * depth : (index + 1) * depth, :].T)
+            left_ref[index, :half] = upper
+            left_ref[index, half:] = lower
+
     acc_ref[...] = jnp.zeros_like(acc_ref)
 
     def step(block, carry):
         rows = pl.ds(pl.multiple_of(block * depth, depth), depth)
-        total = acc_ref[...]
-        for which, tile in enumerate(tiles):
-            total += jnp.dot(
-                left_ref[which, block], tile[rows, :], preferred_element_type=jnp.float32
-            )
-        acc_ref[...] = total
+        shifted = penalty * (
+            est_ref[rows, :].astype(jnp.float32) - dual_ref[rows, :].astype(jnp.float32)
+        ) - cov_ref[rows, :].astype(jnp.float32)
+        upper, lower = split(shifted)
+        acc_ref[...] += jnp.dot(left_ref[block], upper, preferred_element_type=jnp.float32)
+        acc_ref[:half] += jnp.dot(left_ref[block, :half], lower, preferred_element_type=jnp.float32)
         return carry
 
     lax.fori_loop(0, blocks, step, 0)
-    half = acc_ref.shape[0] // 2
-    return acc_ref[:half] + acc_ref[half:]
-
-
-def image_kernel(est_ref, dual_ref, cov_ref, basis_ref, out_ref, left_ref, acc_ref):
-    depth = left_ref.shape[3]
-
-    @pl.when(pl.program_id(0) == 0)
-    def _():
-        for index in range(left_ref.shape[1]):
-            fill_left(left_ref, index, basis_ref[index * depth : (index + 1) * depth, :].T)
-
-    out_ref[0] = shifted_product(left_ref, (est_ref, dual_ref, cov_ref), acc_ref)
-
-
-def moment_kernel(est_ref, dual_ref, cov_ref, rows_ref, cols_ref, out_ref, left_ref, acc_ref):
-    step = pl.program_id(0)
-    rank = rows_ref.shape[1]
-
-    @pl.when(step == 0)
-    def _():
-        for index in range(left_ref.shape[1]):
-            fill_left(left_ref, index, rows_ref[index])
-        own = cols_ref[lax.axis_index("row")]
-        out_ref[:rank] = high_dot(own, own, ((1,), (1,)))
-        out_ref[rank:] = jnp.zeros((rank, rank), jnp.float32)
-
-    image = shifted_product(left_ref, (est_ref, dual_ref, cov_ref), acc_ref)
-    out_ref[rank:] += high_dot(image, cols_ref[step], ((1,), (1,)))
-
-
-def local_call(kernel, matrices, extras, piece, depth, out_shape, out_spec):
+    out_ref[0] = acc_ref[:half] + acc_ref[half:]
+
+
+def image_parts(matrices, start_basis, piece):
     rows_tile, cols_tile = matrices[0].shape
-    rank = 128
-    tile_spec = pl.BlockSpec((rows_tile, piece), lambda step: (0, step))
-    whole = [pl.BlockSpec(extra.shape, functools.partial(lambda n, step: (0,) * n, extra.ndim)) for extra in extras]
-    rank = extras[0].shape[1]
+    rank = start_basis.shape[1]
+    depth = min(256, rows_tile)
     return pl.pallas_call(
-        kernel,
+        image_kernel,
         grid=(cols_tile // piece,),
-        in_specs=[tile_spec] * 3 + whole,
-        out_specs=out_spec,
-        out_shape=out_shape,
+        in_specs=[pl.BlockSpec((rows_tile, piece), lambda step: (0, step))] * 3
+        + [pl.BlockSpec(start_basis.shape, lambda step: (0, 0))],
+        out_specs=pl.BlockSpec((1, rank, piece), lambda step: (step, 0, 0)),
+        out_shape=jax.ShapeDtypeStruct((cols_tile // piece, rank, piece), jnp.float32),
         scratch_shapes=[
-            pltpu.VMEM((3, rows_tile // depth, 2 * rank, depth), jnp.bfloat16),
+            pltpu.VMEM((rows_tile // depth, 2 * rank, depth), jnp.bfloat16),
             pltpu.VMEM((2 * rank, piece), jnp.float32),
         ],
         compiler_params=pltpu.CompilerParams(
             dimension_semantics=("arbitrary",), vmem_limit_bytes=VMEM_BYTES
         ),
-    )(*matrices, *extras)
+    )(*matrices, start_basis)
+
+
+def moment_kernel(est_ref, dual_ref, cov_ref, rows_ref, cols_ref, out_ref, right_ref):
+    count, rank, piece = cols_ref.shape
+
+    @pl.when(pl.program_id(0) == 0)
+    def _():
+        for k in range(count):
+            flat = cols_ref[k].T
+            scaled_upper, scaled_lower = split(penalty * flat)
+            upper, lower = split(flat)
+            right_ref[0, k, :, :rank] = scaled_upper
+            right_ref[0, k, :, rank:] = scaled_lower
+            right_ref[1, k, :, :rank] = -scaled_upper
+            right_ref[1, k, :, rank:] = -scaled_lower
+            right_ref[2, k, :, :rank] = -upper
+            right_ref[2, k, :, rank:] = -lower
+        own = cols_ref[lax.axis_index("row")]
+        out_ref[:rank] = high_dot(own, own, ((1,), (1,)))
+        out_ref[rank:] = jnp.zeros((rank, rank), jnp.float32)
+
+    image = jnp.zeros((est_ref.shape[0], 2 * rank), jnp.float32)
+    for k in range(count):
+        where = slice(k * piece, (k + 1) * piece)
+        for which, tile in enumerate((est_ref, dual_ref, cov_ref)):
+            image += jnp.dot(tile[:, where], right_ref[which, k], preferred_element_type=jnp.float32)
+    out_ref[rank:] += high_dot(rows_ref[0], image[:, :rank] + image[:, rank:], ((1,), (0,)))
+
+
+def moment_terms(matrices, rows, cols):
+    rows_tile, cols_tile = matrices[0].shape
+    count, rank, piece = cols.shape
+    depth = min(256, piece)
+    per = piece // depth
+    return pl.pallas_call(
+        moment_kernel,
+        grid=(rows_tile // depth,),
+        in_specs=[pl.BlockSpec((depth, cols_tile), lambda step: (step, 0))] * 3
+        + [
+            pl.BlockSpec((1, rank, depth), lambda step: (step // per, 0, step % per)),
+            pl.BlockSpec(cols.shape, lambda step: (0, 0, 0)),
+        ],
+        out_specs=pl.BlockSpec((2 * rank, rank), lambda step: (0, 0)),
+        out_shape=jax.ShapeDtypeStruct((2 * rank, rank), jnp.float32),
+        scratch_shapes=[pltpu.VMEM((3, count, piece, 2 * rank), jnp.bfloat16)],
+        compiler_params=pltpu.CompilerParams(
+            dimension_semantics=("arbitrary",), vmem_limit_bytes=VMEM_BYTES
+        ),
+    )(*matrices, rows, cols)
 
 
 def spread_kernel(n_row, n_col, part_ref, mc_ref, mr_ref, near, other, zbuf, sems):
@@ -359,63 +376,77 @@
     )(parts)
 
 
-def total_kernel(n_row, n_col, term_ref, out_ref, terms, send1, recv1, send2, recv2):
-    count = n_row * n_col
+def total_kernel(n_row, n_col, term_ref, out_ref, terms, part, planes, *sems):
+    send1, recv1, send2, recv2, send3, recv3 = sems
     row, col = lax.axis_index("row"), lax.axis_index("col")
-    me = row * n_col + col
     barrier = pltpu.get_barrier_semaphore()
 
-    def place(t):
-        there = (me + t) % count
-        return there, (there // n_col, there % n_col)
-
-    def greet(t, carry):
-        pl.semaphore_signal(barrier, inc=1, device_id=place(t)[1], device_id_type=MESH)
+    def greet_row(t, carry):
+        pl.semaphore_signal(barrier, inc=1, device_id=((row + t) % n_row, col), device_id_type=MESH)
         return carry
 
-    lax.fori_loop(1, count, greet, 0)
-    pl.semaphore_wait(barrier, count - 1)
-
-    def scatter(t):
-        there, target = place(t)
+    def greet_col(t, carry):
+        pl.semaphore_signal(barrier, inc=1, device_id=(row, (col + t) % n_col), device_id_type=MESH)
+        return carry
+
+    lax.fori_loop(1, n_row, greet_row, 0)
+    lax.fori_loop(1, n_col, greet_col, 0)
+    pl.semaphore_wait(barrier, n_row - 1 + n_col - 1)
+
+    def copy(src, dst, send, recv, target):
         return pltpu.make_async_remote_copy(
-            src_ref=term_ref.at[there], dst_ref=terms.at[t], send_sem=send1.at[t],
-            recv_sem=recv1.at[t], device_id=target, device_id_type=MESH,
+            src_ref=src, dst_ref=dst, send_sem=send, recv_sem=recv, device_id=target, device_id_type=MESH
         )
 
-    def gather(t, slot):
-        return pltpu.make_async_remote_copy(
-            src_ref=out_ref.at[me], dst_ref=out_ref.at[slot], send_sem=send2.at[t],
-            recv_sem=recv2.at[t], device_id=place(t)[1], device_id_type=MESH,
-        )
-
-    def each(action):
-        def step(t, carry):
-            action(t)
-            return carry
-
-        lax.fori_loop(1, count, step, 0)
-
-    each(lambda t: scatter(t).start())
-    terms[0] = term_ref[me]
-    each(lambda t: scatter(t).wait_recv())
-    out_ref[me] = jnp.sum(terms[...], axis=0)
-    each(lambda t: gather(t, me).start())
-    each(lambda t: gather(t, (me + count - t) % count).wait_recv())
-    each(lambda t: scatter(t).wait_send())
-    each(lambda t: gather(t, me).wait_send())
+    first = []
+    for t in range(1, n_row):
+        there = (row + t) % n_row
+        first.append(copy(term_ref.at[there], terms.at[t], send1.at[t], recv1.at[t], (there, col)))
+        first[-1].start()
+    summed = term_ref[row]
+    for t in range(1, n_row):
+        first[t - 1].wait_recv()
+        summed += terms[t]
+    part[...] = summed
+    second = []
+    for t in range(1, n_col):
+        there = (col + t) % n_col
+        second.append(copy(part, planes.at[col], send2.at[t], recv2.at[col], (row, there)))
+        second[-1].start()
+    planes[col] = summed
+    for t in range(1, n_col):
+        source = (col + t) % n_col
+        copy(part, planes.at[source], send2.at[t], recv2.at[source], (row, source)).wait_recv()
+    out_ref[row] = jnp.sum(planes[...], axis=0)
+    third = []
+    for t in range(1, n_row):
+        there = (row + t) % n_row
+        third.append(copy(out_ref.at[row], out_ref.at[row], send3.at[t], recv3.at[t], (there, col)))
+        third[-1].start()
+    for t in range(1, n_row):
+        source = (row + n_row - t) % n_row
+        copy(out_ref.at[row], out_ref.at[source], send3.at[t], recv3.at[t], (source, col)).wait_recv()
+    for item in first + second + third:
+        item.wait_send()
 
 
 def total(terms, n_row, n_col):
-    count = n_row * n_col
-    blocks = terms.reshape(count, terms.shape[0] // count, terms.shape[1])
+    blocks = terms.reshape(n_row, terms.shape[0] // n_row, terms.shape[1])
+    block = blocks.shape[1:]
     dma = pltpu.SemaphoreType.DMA
     summed = pl.pallas_call(
         functools.partial(total_kernel, n_row, n_col),
         in_specs=[VMEM],
         out_specs=VMEM,
         out_shape=jax.ShapeDtypeStruct(blocks.shape, jnp.float32),
-        scratch_shapes=[pltpu.VMEM(blocks.shape, jnp.float32)] + [dma((count,))] * 4,
+        scratch_shapes=[
+            pltpu.VMEM(blocks.shape, jnp.float32),
+            pltpu.VMEM(block, jnp.float32),
+            pltpu.VMEM((n_col, *block), jnp.float32),
+            dma((n_row,)), dma((n_row,)),
+            dma((n_col,)), dma((n_col,)),
+            dma((n_row,)), dma((n_row,)),
+        ],
         compiler_params=pltpu.CompilerParams(collective_id=1, has_side_effects=True),
     )(blocks)
     return summed.reshape(terms.shape)
@@ -497,7 +528,7 @@
 def finish(weighted, cols, dual_var):
     rows_tile, cols_tile = dual_var.shape
     count, rank, piece = cols.shape
-    depth = min(256, rows_tile)
+    depth = min(512, rows_tile)
     wide = pl.BlockSpec((depth, cols_tile), lambda step: (step, 0))
     return pl.pallas_call(
         finish_kernel,
@@ -527,17 +558,9 @@
     rank = start_basis.shape[1]
     piece = cols_tile // n_row
     matrices = (estimate, dual_var, covariance)
-    parts = local_call(
-        image_kernel, matrices, (start_basis,), piece, piece,
-        jax.ShapeDtypeStruct((n_row, rank, piece), jnp.float32),
-        pl.BlockSpec((1, rank, piece), lambda step: (step, 0, 0)),
-    )
+    parts = image_parts(matrices, start_basis, piece)
     cols, rows = spread(parts, n_row, n_col)
-    moments = local_call(
-        moment_kernel, matrices, (rows, cols), piece, piece,
-        jax.ShapeDtypeStruct((2 * rank, rank), jnp.float32),
-        pl.BlockSpec((2 * rank, rank), lambda step: (0, 0)),
-    )
+    moments = moment_terms(matrices, rows, cols)
     moments = total(moments, n_row, n_col)
     weighted = pl.pallas_call(
         weight_kernel,
@@ -562,7 +585,7 @@
         and piece % 128 == 0
         and rows_tile % piece == 0
         and rank % 128 == 0
-        and 2 * rank % (8 * n_row * n_col) == 0
+        and 2 * rank % (8 * n_row) == 0
     )
     if not fits:
         return plain_body(covariance, estimate, dual_var, start_basis)

time: 179 us -> 175 us (0.978)
  Pallas kernels: 177 us -> 174 us
    pallas_call x1, Pallas kernels: 23.7 us -> 20.7 us  [total(): pl.pallas_call(functools.partial(total_kernel, n_row, n_col), in_specs=[V...]
where the time goes in v1:
time: 175 us
  Pallas kernels  174 us (99%)
    pallas_call x1, Pallas kernels, spread(): pl.pallas_call(kernel, in_specs=[VMEM], out_specs=(VMEM, VMEM), out_shape...  53.5 us
    pallas_call x1, Pallas kernels, image_parts(): pl.pallas_call(image_kernel, grid=(cols_tile // piece,), in_specs=[pl.Blo...  28.7 us
    pallas_call x1, Pallas kernels, moment_terms(): pl.pallas_call(moment_kernel, grid=(rows_tile // depth,), in_specs=[pl.Bl...  26.1 us
    pallas_call x1, Pallas kernels, finish(): pl.pallas_call(finish_kernel, grid=(rows_tile // depth,), in_specs=[pl.Bl...  24.6 us
    pallas_call x1, Pallas kernels, total(): pl.pallas_call(functools.partial(total_kernel, n_row, n_col), in_specs=[V...  20.7 us
    pallas_call x1, Pallas kernels, fast_body(): pl.pallas_call(weight_kernel, in_specs=[VMEM, VMEM], out_specs=VMEM, out_...  20.4 us

profile of v1, /device:TPU:0, one launch (start us, length us, event | category | flops | bytes accessed | tf_op | source)
XLA Modules:
  0.0 174.5 jit_solution(11706043899344867150)
XLA Ops:
  0.6 28.7 %shard_map.59.part_ref = f32[8,128,512]{2,1,0:T(8,128)} custom-call(bf16[2048,4096]{1,0:T(8,128)(2,1)} %est_ref.3, bf16[2048,4096]{1,0:T(8,128)(2,1)} %dual_ref.5, bf16[2048,4096]{1,0:T(8,128)(2,1)} %cov_ref.3, f32[2048,128]{1,0:T(8,128)} %basis_ref.1), custom_call_target="tpu_custom_call" | custom-call | tf_op jit(solution)/shard_map/pallas_call | solution.py:168
  29.3 53.5 %shard_map.60 = (f32[8,128,512]{2,1,0:T(8,128)}, f32[4,128,512]{2,1,0:T(8,128)}) custom-call(f32[8,128,512]{2,1,0:T(8,128)} %shard_map.59.part_ref), custom_call_target="tpu_custom_call" | custom-call | tf_op jit(solution)/shard_map/pallas_call | solution.py:354
  82.8 26.1 %shard_map.61 = f32[256,128]{1,0:T(8,128)} custom-call(bf16[2048,4096]{1,0:T(8,128)(2,1)} %est_ref.3, bf16[2048,4096]{1,0:T(8,128)(2,1)} %dual_ref.5, bf16[2048,4096]{1,0:T(8,128)(2,1)} %cov_ref.3, f32[4,128,512]{2,1,0:T(8,128)} %get-tuple-element.4.rows_ref, f32[8,128,512]{2,1,0:T(8,128)} %get-tuple-element.5.cols_ref), custom_call_target="tpu_custom_call" | custom-call | tf_op jit(solution)/shard_map/pallas_call | solution.py:217
  108.9 20.7 %shard_map.62 = f32[8,32,128]{2,1,0:T(8,128)} custom-call(f32[8,32,128]{2,1,0:T(8,128)} %bitcast.2), custom_call_target="tpu_custom_call" | custom-call | tf_op jit(solution)/shard_map/pallas_call | solution.py:437
  129.6 20.4 %shard_map.63.weighted_ref = f32[2048,128]{1,0:T(8,128)} custom-call(f32[256,128]{1,0:T(8,128)} %bitcast.3, f32[4,128,512]{2,1,0:T(8,128)} %get-tuple-element.4.rows_ref), custom_call_target="tpu_custom_call" | custom-call | tf_op jit(solution)/shard_map/pallas_call | solution.py:565
  150.0 24.6 %shard_map.64 = (f32[2048,4096]{1,0:T(8,128)}, bf16[2048,4096]{1,0:T(8,128)(2,1)}) custom-call(f32[2048,128]{1,0:T(8,128)} %shard_map.63.weighted_ref, f32[8,128,512]{2,1,0:T(8,128)} %get-tuple-element.5.cols_ref, bf16[2048,4096]{1,0:T(8,128)(2,1)} %dual_ref.5), custom_call_target="tpu_custom_call" | custom-call | tf_op jit(solution)/shard_map/pallas_call | solution.py:533
